TPU v7x, 512 devices: a 8x2x16 block of a 8x8x16 slice. The times are simulated.
512 devices in a mesh: grp: 2 (over y), dp: 256 (over z, x, core).
Axes of the slice: x: 8, y: 2, z: 16, core: 2. Of those that a mesh axis runs over, the one named last changes fastest.
The devices are a block of a 8x8x16 slice.
Arguments:
- params: float32 [1900544], P(('grp', 'dp')), parts along dimension 0, may hold values from -0.3 to 0.3
- momentum: float32 [1900544], P(('grp', 'dp')), parts along dimension 0, may hold values from -6 to 6
- noise_draws: float32 [2, 950272], P('grp', 'dp'), parts along dimension 0, may hold values from -6 to 6
- images: float32 [262144, 448], P(('grp', 'dp')), parts along dimension 0, may hold values from -6 to 6
- labels: int32 [262144], P(('grp', 'dp')), parts along dimension 0, may hold values from 0 to 9
- indices: int32 [2, 65536], P('grp', 'dp'), parts along dimension 0, may hold values from 0 to 511
Outputs:
- params_out: float32 [1900544], P(('grp', 'dp')), parts along dimension 0
- momentum_out: float32 [1900544], P(('grp', 'dp')), parts along dimension 0
- losses: float32 [2], P('grp'), parts along dimension 0
There are 2 independent parts, one for each index of `grp`. A program takes and returns all parts, laid end to end along the dimension named above; each array names one. Nothing has to cross between parts.
All inputs are finite; a program needn't handle non-finite values.
Results may differ from a plain program's by a relative error of at most 0.0003.
Values sent between devices are 32-bit elements; how exact they have to be, the bound alone decides.
A program may use at most 64 MiB of HBM per device.

v0:
```python
import math
import jax
import jax.numpy as jnp
from jax import lax
from jax.sharding import Mesh
from jax.sharding import PartitionSpec as P

DIN = 448
H = 2048
OUT = 10
DP = ("dp_0", "dp_1", "dp_2")
GRP_DP = ("grp", "dp_0", "dp_1", "dp_2")
step_size = 0.02
friction = 15.0


def laid_out(parts, dim):
    dims = list(parts.shape[1:])
    dims[dim] *= parts.shape[0]
    return jnp.moveaxis(parts, 0, dim).reshape(dims)


def gather_in_order(value, axes, turns):
    parts = value[None]
    for k in turns:
        parts = lax.all_gather(parts, axes[k], axis=0, tiled=True)
    block = [lax.axis_size(axes[k]) for k in reversed(turns)]
    parts = parts.reshape(*block, *value.shape)
    turned = sorted(range(len(turns)), key=lambda place: turns[len(turns) - 1 - place])
    return parts.transpose(*turned, *range(len(turns), parts.ndim)).reshape(-1, *value.shape)


def gathered_by_axis(value, axes, turns, dim):
    return laid_out(gather_in_order(value, axes, turns), dim)


def one_axis_at_a_time(value, axes):
    for axis in axes:
        value = lax.psum(value, axis)
    return value


def own_block(parts, axes, turns):
    dims = [lax.axis_size(a) for a in axes]
    parts = parts.reshape(*dims, *parts.shape[1:])
    parts = parts.transpose(*turns, *range(len(axes), parts.ndim))
    parts = parts.reshape(-1, *parts.shape[len(axes) :])
    for k in turns:
        parts = lax.psum_scatter(parts, axes[k], scatter_dimension=0, tiled=True)
    return parts[0]


def cut_along(value, dim, size):
    before, after = (value.shape[:dim], value.shape[dim + 1 :])
    return jnp.moveaxis(value.reshape(*before, size, -1, *after), dim, 0)


def scatter_axes(value, axes, turns, dim):
    size = lax.axis_size(axes)
    return own_block(cut_along(value, dim, size), axes, turns)


def unpack(flat_vec):
    in_end = DIN * H
    w_in = flat_vec[:in_end].reshape(DIN, H)
    b_in = flat_vec[in_end : in_end + H]
    hid_end = in_end + H
    w_out = flat_vec[hid_end : hid_end + H * OUT].reshape(H, OUT)
    b_out = flat_vec[hid_end + H * OUT : hid_end + H * OUT + OUT]
    return (w_in, b_in, w_out, b_out)


def total_nll(flat_vec, chosen_rows, targets):
    w_in, b_in, w_out, b_out = unpack(flat_vec)
    hidden = jnp.tanh(
        jnp.dot(
            chosen_rows, w_in, precision=lax.Precision.HIGHEST, preferred_element_type=jnp.float32
        )
        + b_in
    )
    logits = (
        jnp.dot(hidden, w_out, precision=lax.Precision.HIGHEST, preferred_element_type=jnp.float32)
        + b_out
    )
    log_norm = jnp.log(jnp.sum(jnp.exp(logits), axis=1))
    classes = lax.broadcasted_iota(jnp.int32, logits.shape, 1)
    picked = jnp.sum(jnp.where(targets[:, None] == classes, logits, 0.0), axis=1)
    return jnp.sum(log_norm - picked)


def prior_precision(flat_index):
    in_end = DIN * H
    hid_end = in_end + H
    out_end = hid_end + H * OUT
    return jnp.where(
        flat_index < in_end,
        float(DIN),
        jnp.where(flat_index < hid_end, 1.0, jnp.where(flat_index < out_end, float(H), 1.0)),
    )


def body(params, momentum, noise_draws, images, labels, indices):
    shard_len = params.shape[0]
    shard_start = lax.axis_index(DP) * shard_len
    precision = prior_precision(shard_start + lax.iota(jnp.int32, shard_len))
    scale_data = images.shape[0] / indices.shape[1]
    row_count = lax.axis_size(DP) * indices.shape[1]
    gathered = gathered_by_axis(params, DP, (0, 1, 2), 0)
    picked_rows = indices[0]
    chosen_rows = jnp.take(images, picked_rows, axis=0)
    targets = jnp.take(labels, picked_rows, axis=0)
    nll_part, pullback = jax.vjp(
        lambda weights_flat: total_nll(weights_flat, chosen_rows, targets), gathered
    )
    (local_grad,) = pullback(jnp.ones_like(nll_part))
    losses = [one_axis_at_a_time(nll_part, DP) / row_count]
    own_grad = scatter_axes(local_grad, DP, (2, 0, 1), 0)
    total_force = scale_data * own_grad + precision * params
    momentum = (
        (1.0 - step_size * friction) * momentum
        - step_size * total_force
        + math.sqrt(2.0 * friction * step_size) * noise_draws[0]
    )
    params = params + step_size * momentum
    return (params, momentum, jnp.stack(losses))


def solution(mesh):
    torus = Mesh(mesh.devices.reshape(mesh.shape["grp"], 16, 8, 2), ("grp", "dp_0", "dp_1", "dp_2"))
    placed = (P(GRP_DP), P(GRP_DP), P("grp", DP), P(GRP_DP, None), P(GRP_DP), P("grp", DP))
    return jax.shard_map(
        body,
        mesh=torus,
        in_specs=placed,
        out_specs=(P(GRP_DP), P(GRP_DP), P("grp")),
        check_vma=False,
    )
```

profile of v0, /device:TPU:66, one launch (start us, length us, event | category | flops | bytes accessed | tf_op | source)
XLA Modules:
  0.0 469.8 jit_solution(17000663822888148046)
XLA Ops:
  7.2 0.0 copy-start
  7.2 0.0 copy-start.1
  7.2 0.1 all-gather.5.cloned.1.call-start
  7.3 0.8 reshape.105
  8.1 69.3 %all-gather.1 = f32[16,1,3712]{2,1,0:T(1,128)S(1)} all-gather(f32[1,1,3712]{2,1,0:T(1,128)S(1)} %reshape.105), channel_id=2, replica_groups=mesh['grp'=2,'dp_0'=16,'dp_1'=8,'dp_2'=2] {'dp_0'}, dimensions={0}, use_global_device_ids=true | all-gather | bytes 252416 | tf_op jit(solution)/shard_map/all_gather | solution.py:26
  77.4 0.7 copy.26
  78.1 0.0 copy-start.5
  78.1 0.1 all-gather.5.cloned.1.call-update
  78.2 0.1 all-gather.7.cloned.1.call-start
  78.3 40.2 %all-gather.5.cloned.1.call-done = f32[128,3712]{1,0:T(8,128)} async-done(((f32[16,3712]{1,0:T(8,128)}), f32[128,3712]{1,0:T(8,128)}) %all-gather.5.cloned.1.call-update) | async-done | bytes 1900560 | tf_op jit(solution)/shard_map/all_gather | solution.py:26
  118.4 0.1 all-gather.7.cloned.1.call-update
  118.5 0.1 reduce-scatter.2.cloned.1.call-start
  118.6 0.0 copy-done.1
  118.6 0.3 copy.17
  118.9 0.0 copy-done.5
  119.0 1.0 gather_fusion.1
  119.9 0.0 copy-done
  119.9 1.9 gather_fusion
  121.9 22.7 %all-gather.7.cloned.1.call-done = f32[256,3712]{1,0:T(8,128)} async-done(((f32[128,3712]{1,0:T(8,128)}), f32[256,3712]{1,0:T(8,128)}) %all-gather.7.cloned.1.call-update) | async-done | bytes 3801104 | tf_op jit(solution)/shard_map/all_gather | solution.py:26
  144.6 6.8 %copy.18 = f32[16,8,2,3712]{3,2,1,0:T(2,128)} copy(f32[16,8,2,3712]{3,0,1,2:T(8,128)} %bitcast.26) | data formatting | bytes 7602176 | tf_op jit(solution)/shard_map/transpose | solution.py:30
  151.5 5.8 %slice.15 = f32[464,2048]{1,0:T(8,128)} reshape(f32[16,8,2,3712]{3,2,1,0:T(2,128)} %copy.18) | data formatting | bytes 7602176 | tf_op jit(solution)/shard_map/jvp()/slice | solution.py:65
  157.3 5.9 %reshape_reshape.6 = f32[950272]{0:T(1024)} reshape(f32[16,8,2,3712]{3,2,1,0:T(2,128)} %copy.18) | data formatting | bytes 7602176 | tf_op jit(solution)/shard_map/reshape;reshape | solution.py:20
  163.2 0.7 slice.25
  163.9 0.9 slice.26
  164.8 1.1 reshape.84
  165.9 0.0 slice-start
  165.9 5.7 %fusion.5 = f32[256,2048]{1,0:T(8,128)S(1)} fusion(f32[464,2048]{1,0:T(8,128)} %slice.15, f32[2048]{0:T(1024)S(1)} %slice.25, f32[256,448]{1,0:T(8,128)S(1)} %gather_fusion.1, pred[256]{0:T(512)(128)(4,1)S(1)} %get-tuple-element.8), kind=kOutput, calls=%fused_computation.6 | convolution fusion | flops 2819211264 | bytes 6234368 | tf_op jit(solution)/shard_map/jvp()/dot_general | solution.py:76
  171.6 0.0 slice-done
  171.6 1.9 exponential_reduce_fusion
  173.5 2.1 fusion.26
  175.6 3.6 fusion.18
  179.2 0.1 select_reduce_fusion
  179.4 3.6 convolution_bitcast_fusion
  183.0 2.6 copy.24
  185.6 0.8 reshape.85
  186.4 4.1 pad_add_fusion
  190.5 5.5 %reshape_reshape.7 = f32[16,8,2,3712]{3,2,1,0:T(2,128)} reshape(f32[950272]{0:T(1024)} %pad_add_fusion) | data formatting | bytes 7602176 | tf_op jit(solution)/shard_map/reshape;reshape | solution.py:45
  196.0 4.1 copy.21
  200.1 0.1 reduce-scatter.2.cloned.1.call-update
  200.2 0.0 copy-start.4
  200.2 0.0 copy-start.2
  200.2 0.0 copy-start.3
  200.2 0.1 all-reduce.9.cloned.1.call-start
  200.3 25.6 %reduce-scatter.2.cloned.1.call-done = f32[128,3712]{1,0:T(8,128)} async-done(((f32[256,3712]{1,0:T(8,128)}), f32[128,3712]{1,0:T(8,128)}) %reduce-scatter.2.cloned.1.call-update) | async-done | bytes 1900560 | tf_op jit(solution)/shard_map/reduce_scatter | solution.py:49
  225.9 0.1 all-reduce.9.cloned.1.call-update
  225.9 0.1 all-reduce.11.cloned.1.call-start
  226.0 1.3 dynamic-slice
  227.9 148.8 %all-reduce.9.cloned.1.call-done = f32[128,3712]{1,0:T(8,128)} async-done(((f32[128,3712]{1,0:T(8,128)}), f32[128,3712]{1,0:T(8,128)}) %all-reduce.9.cloned.1.call-update) | async-done | bytes 1900560
  376.7 1.6 constant_dynamic-slice_fusion
  378.2 0.1 all-reduce.11.cloned.1.call-update
  378.3 0.0 copy-done.4
  378.4 1.3 dynamic-slice.2
  379.6 0.6 subtract_reduce_fusion
  380.2 29.9 %psum.21 = f32[]{:T(128)} all-reduce(f32[]{:T(128)} %subtract_reduce_fusion), channel_id=1, replica_groups=mesh['grp'=2,'dp_0'=16,'dp_1'=8,'dp_2'=2] {'dp_0'}, use_global_device_ids=true, to_apply=%region_8.9 | all-reduce | flops 1 | bytes 8 | tf_op jit(solution)/shard_map/psum | solution.py:39
  410.1 16.3 %psum.22 = f32[]{:T(128)} all-reduce(f32[]{:T(128)} %psum.21), channel_id=1, replica_groups=mesh['grp'=2,'dp_0'=16,'dp_1'=8,'dp_2'=2] {'dp_1'}, use_global_device_ids=true, to_apply=%region_9.10 | all-reduce | flops 1 | bytes 8 | tf_op jit(solution)/shard_map/psum | solution.py:39
  426.4 3.1 psum.23
  430.2 29.6 %all-reduce.11.cloned.1.call-done = f32[8,3712]{1,0:T(8,128)} async-done(((f32[8,3712]{1,0:T(8,128)}), f32[8,3712]{1,0:T(8,128)}) %all-reduce.11.cloned.1.call-update) | async-done | bytes 118800
  459.8 1.6 fusion.17
  461.4 0.0 copy-done.2
  461.4 0.0 copy-done.3
  461.5 0.6 multiply_add_fusion
  (5 shorter events, 0.1 us)
Async XLA Ops:
  7.2 112.7 %copy-start = (s32[512]{0:T(512)S(1)}, s32[512]{0:T(512)}, u32[]{:S(2)}) copy-start(s32[512]{0:T(512)} %param.10) | copy-start | bytes 6148
  7.2 111.4 %copy-start.1 = (f32[512,448]{0,1:T(8,128)S(1)}, f32[512,448]{0,1:T(8,128)}, u32[]{:S(2)}) copy-start(f32[512,448]{0,1:T(8,128)} %param.9) | copy-start | bytes 2752516
  7.2 111.2 %all-gather.5.cloned.1.call-start = ((), (), s32[]{:S(2)}) async-start(), calls=%async_computation.1 | async-start | bytes 2138112 | tf_op jit(solution)/shard_map/all_gather | solution.py:26
  78.1 40.8 %copy-start.5 = (s32[1,256]{1,0:T(1,128)S(1)}, s32[1,256]{1,0:T(1,128)}, u32[]{:S(2)}) copy-start(s32[1,256]{1,0:T(1,128)} %param.11) | copy-start | bytes 3076
  78.2 66.5 %all-gather.7.cloned.1.call-start = ((), (), s32[]{:S(2)}) async-start(), calls=%async_computation.2 | async-start | bytes 5701632 | tf_op jit(solution)/shard_map/all_gather | solution.py:26
  118.5 107.4 %reduce-scatter.2.cloned.1.call-start = ((), (), s32[]{:S(2)}) async-start(), calls=%async_computation.3 | async-start | bytes 5701632 | tf_op jit(solution)/shard_map/reduce_scatter | solution.py:49
  165.9 5.7 %slice-start = ((f32[950272]{0:T(1024)}), f32[10]{0:T(128)S(1)}, s32[]{:S(2)}) async-start(f32[950272]{0:T(1024)} %reshape_reshape.6), calls=%async_computation.6 | async-start | bytes 1024 | tf_op jit(solution)/shard_map/jvp()/slice | solution.py:69
  200.2 178.1 %copy-start.4 = (f32[1,3712]{1,0:T(1,128)S(1)}, f32[1,3712]{1,0:T(1,128)}, u32[]{:S(2)}) copy-start(f32[1,3712]{1,0:T(1,128)} %param.8) | copy-start | bytes 44548
  200.2 261.3 %copy-start.2 = (f32[3712]{0:T(1024)S(1)}, f32[3712]{0:T(1024)}, u32[]{:S(2)}) copy-start(f32[3712]{0:T(1024)} %param.6) | copy-start | bytes 44548
  200.2 261.3 %copy-start.3 = (f32[3712]{0:T(1024)S(1)}, f32[3712]{0:T(1024)}, u32[]{:S(2)}) copy-start(f32[3712]{0:T(1024)} %param.7) | copy-start | bytes 44548
  200.2 176.5 %all-reduce.9.cloned.1.call-start = ((), (), s32[]{:S(2)}) async-start(), calls=%async_computation.4 | async-start | bytes 3801088
  225.9 233.9 %all-reduce.11.cloned.1.call-start = ((), (), s32[]{:S(2)}) async-start(), calls=%async_computation.5 | async-start | bytes 237568
Sparse Core Ops, SparseCore 0:
  78.3 40.0 all-gather.4
  120.5 24.0 all-gather.6
  200.3 25.5 reduce-scatter.1
  228.1 148.4 all-reduce.8
  378.9 80.9 all-reduce.10
where the time goes:
time: 470 us
  waiting for transfers between devices  267 us (57%)
  blocking collectives  119 us (25%)
  local copies, waits for them, and re-layouts  43.1 us (9%)
  matrix products  16.9 us (4%)
  between operations  16.5 us (4%)
  other arithmetic  7.13 us (2%)
    unnamed x7, waiting for transfers between devices  179 us
    all_gather x1, blocking collectives, gather_in_order(): parts = lax.all_gather(parts, axes[k], axis=0, tiled=True)  69.3 us
    all_gather x2, waiting for transfers between devices, gather_in_order(): parts = lax.all_gather(parts, axes[k], axis=0, tiled=True)  62.9 us
    psum x3, blocking collectives, one_axis_at_a_time(): value = lax.psum(value, axis)  49.3 us
    reduce_scatter x1, waiting for transfers between devices, own_block(): parts = lax.psum_scatter(parts, axes[k], scatter_dimension=0, tiled=True)  25.6 us
  transfers between devices with their start and end apart: 5, of which 5 were waited for; matrix products, arithmetic and copies ran while one was open for 1% of the time, Pallas kernels for 0%

commit v1 on v0

--- a/solution.py
+++ b/solution.py
@@ -23,7 +23,9 @@
 def gather_in_order(value, axes, turns):
     parts = value[None]
     for k in turns:
-        parts = lax.all_gather(parts, axes[k], axis=0, tiled=True)
+        parts = jnp.concatenate(
+            lax.all_to_all(jnp.stack([parts] * lax.axis_size(axes[k])), axes[k], 0, 0), axis=0
+        )
     block = [lax.axis_size(axes[k]) for k in reversed(turns)]
     parts = parts.reshape(*block, *value.shape)
     turned = sorted(range(len(turns)), key=lambda place: turns[len(turns) - 1 - place])

time: 470 us -> 445 us (0.947)
  waiting for transfers between devices: 267 us -> 236 us
  starting transfers between devices: 0.31 us -> 7.97 us
    all_gather x1 -> x0, blocking collectives: 69.3 us -> none  [gather_in_order(): parts = lax.all_gather(parts, axes[k], axis=0, tiled=True)]
    all_to_all x0 -> x2, blocking collectives: none -> 67.7 us  [gather_in_order(): lax.all_to_all(jnp.stack([parts] * lax.axis_size(axes[k])), axes[k], 0, 0)]
    all_gather x2 -> x0, waiting for transfers between devices: 62.9 us -> none  [gather_in_order(): parts = lax.all_gather(parts, axes[k], axis=0, tiled=True)]
    all_to_all x0 -> x1, waiting for transfers between devices: none -> 36.5 us  [gather_in_order(): lax.all_to_all(jnp.stack([parts] * lax.axis_size(axes[k])), axes[k], 0, 0)]
    all_to_all x0 -> x1, starting transfers between devices: none -> 7.84 us  [gather_in_order(): lax.all_to_all(jnp.stack([parts] * lax.axis_size(axes[k])), axes[k], 0, 0)]
    reduce_scatter x1, waiting for transfers between devices: 25.6 us -> 20.1 us  [own_block(): parts = lax.psum_scatter(parts, axes[k], scatter_dimension=0, tiled=True)]
    unnamed x7 -> x5, waiting for transfers between devices: 179 us -> 179 us
  transfers between devices with their start and end apart: 5 -> 4, of which waited for: 5 -> 4; matrix products, arithmetic and copies ran while one was open for 1% -> 2% of each run, Pallas kernels for 0% -> 0%
where the time goes in v1:
time: 445 us; the launch traced here: 444 us
  waiting for transfers between devices  236 us (53%)
  blocking collectives  117 us (26%)
  local copies, waits for them, and re-layouts  43 us (10%)
  matrix products  16.9 us (4%)
  between operations  16.4 us (4%)
  starting transfers between devices  7.97 us (2%)
  other arithmetic  7.38 us (2%)
    unnamed x5, waiting for transfers between devices  179 us
    all_to_all x2, blocking collectives, gather_in_order(): lax.all_to_all(jnp.stack([parts] * lax.axis_size(axes[k])), axes[k], 0, 0)  67.7 us
    psum x3, blocking collectives, one_axis_at_a_time(): value = lax.psum(value, axis)  49.3 us
    all_to_all x1, waiting for transfers between devices, gather_in_order(): lax.all_to_all(jnp.stack([parts] * lax.axis_size(axes[k])), axes[k], 0, 0)  36.5 us
    reduce_scatter x1, waiting for transfers between devices, own_block(): parts = lax.psum_scatter(parts, axes[k], scatter_dimension=0, tiled=True)  20.1 us
    dot_general x2, matrix products, total_nll(): jnp.dot(chosen_rows, w_in, precision=lax.Precision.HIGHEST, preferred_ele...  9.32 us
  transfers between devices with their start and end apart: 4, of which 4 were waited for; matrix products, arithmetic and copies ran while one was open for 2% of the time, Pallas kernels for 0%

profile of v1, /device:TPU:66, one launch (start us, length us, event | category | flops | bytes accessed | tf_op | source)
XLA Modules:
  0.0 444.4 jit_solution(14905619418884683783)
XLA Ops:
  7.2 0.0 copy-start
  7.2 0.8 stack.12
  8.0 60.9 %all_to_all.15 = f32[16,1,3712]{2,1,0:T(1,128)S(1)} all-to-all(f32[16,1,3712]{2,1,0:T(1,128)S(1)} %stack.12), channel_id=1, replica_groups=mesh['grp'=2,'dp_0'=16,'dp_1'=8,'dp_2'=2] {'dp_0'}, dimensions={0} | all-to-all | bytes 475136 | tf_op jit(solution)/shard_map/all_to_all | solution.py:27
  68.9 1.4 stack.13
  70.3 0.0 copy-start.4
  70.3 7.8 %all-to-all-start.1 = ((f32[8,16,3712]{2,1,0:T(8,128)}), f32[8,16,3712]{2,1,0:T(8,128)S(1)}, u32[]{:S(2)}, u32[]{:S(2)}) async-start(f32[8,16,3712]{2,1,0:T(8,128)} %stack.13), calls=%async_computation.1 | async-start | bytes 3801088 | tf_op jit(solution)/shard_map/all_to_all | solution.py:27
  78.2 0.0 reduce-scatter.2.cloned.1.call-start
  78.2 1.5 copy.17
  79.7 0.0 copy-done.4
  79.7 1.0 gather_fusion.1
  80.7 0.0 copy-done
  80.7 1.9 gather_fusion
  82.7 36.5 %all-to-all-done.1 = f32[8,16,3712]{2,1,0:T(8,128)S(1)} async-done(((f32[8,16,3712]{2,1,0:T(8,128)}), f32[8,16,3712]{2,1,0:T(8,128)S(1)}, u32[]{:S(2)}, u32[]{:S(2)}) %all-to-all-start.1) | async-done | bytes 1900576 | tf_op jit(solution)/shard_map/all_to_all | solution.py:27
  119.2 0.2 pad_maximum_fusion
  119.4 6.8 %all_to_all.16 = f32[2,128,3712]{2,1,0:T(8,128)S(1)} all-to-all(f32[2,128,3712]{2,1,0:T(8,128)S(1)} %pad_maximum_fusion), channel_id=1, replica_groups=mesh['grp'=2,'dp_0'=16,'dp_1'=8,'dp_2'=2] {'dp_2'}, dimensions={0} | all-to-all | bytes 7602176 | tf_op jit(solution)/shard_map/all_to_all | solution.py:27
  126.2 4.8 %copy.18 = f32[16,8,2,3712]{3,2,1,0:T(2,128)} copy(f32[16,8,2,3712]{3,0,1,2:T(8,128)S(1)} %bitcast.25) | data formatting | bytes 7602176 | tf_op jit(solution)/shard_map/transpose | solution.py:32
  131.0 5.8 %slice.15 = f32[464,2048]{1,0:T(8,128)} reshape(f32[16,8,2,3712]{3,2,1,0:T(2,128)} %copy.18) | data formatting | bytes 7602176 | tf_op jit(solution)/shard_map/jvp()/slice | solution.py:67
  136.8 5.9 %reshape_reshape.10 = f32[950272]{0:T(1024)} reshape(f32[16,8,2,3712]{3,2,1,0:T(2,128)} %copy.18) | data formatting | bytes 7602176 | tf_op jit(solution)/shard_map/reshape;reshape | solution.py:20
  142.8 0.7 slice.25
  143.5 0.9 slice.26
  144.4 1.1 reshape.84
  145.4 0.0 slice-start
  145.4 5.7 %fusion.5 = f32[256,2048]{1,0:T(8,128)S(1)} fusion(f32[464,2048]{1,0:T(8,128)} %slice.15, f32[2048]{0:T(1024)S(1)} %slice.25, f32[256,448]{1,0:T(8,128)S(1)} %gather_fusion.1, pred[256]{0:T(512)(128)(4,1)S(1)} %get-tuple-element.8), kind=kOutput, calls=%fused_computation.7 | convolution fusion | flops 2819211264 | bytes 6234368 | tf_op jit(solution)/shard_map/jvp()/dot_general | solution.py:78
  151.1 0.0 slice-done
  151.2 1.9 exponential_reduce_fusion
  153.0 2.1 fusion.26
  155.1 3.6 fusion.18
  158.8 0.1 select_reduce_fusion
  158.9 3.6 convolution_bitcast_fusion
  162.5 2.6 copy.24
  165.1 0.8 reshape.85
  165.9 4.1 pad_add_fusion
  170.0 5.5 %reshape_reshape.11 = f32[16,8,2,3712]{3,2,1,0:T(2,128)} reshape(f32[950272]{0:T(1024)} %pad_add_fusion) | data formatting | bytes 7602176 | tf_op jit(solution)/shard_map/reshape;reshape | solution.py:47
  175.5 4.1 copy.21
  179.6 0.1 reduce-scatter.2.cloned.1.call-update
  179.7 0.0 copy-start.3
  179.7 0.0 copy-start.1
  179.7 0.0 copy-start.2
  179.7 0.1 all-reduce.9.cloned.1.call-start
  179.8 20.1 %reduce-scatter.2.cloned.1.call-done = f32[128,3712]{1,0:T(8,128)} async-done(((f32[256,3712]{1,0:T(8,128)}), f32[128,3712]{1,0:T(8,128)}) %reduce-scatter.2.cloned.1.call-update) | async-done | bytes 1900560 | tf_op jit(solution)/shard_map/reduce_scatter | solution.py:51
  199.9 0.1 all-reduce.9.cloned.1.call-update
  199.9 0.1 all-reduce.11.cloned.1.call-start
  200.0 1.3 dynamic-slice
  201.9 149.2 %all-reduce.9.cloned.1.call-done = f32[128,3712]{1,0:T(8,128)} async-done(((f32[128,3712]{1,0:T(8,128)}), f32[128,3712]{1,0:T(8,128)}) %all-reduce.9.cloned.1.call-update) | async-done | bytes 1900560
  351.1 1.6 constant_dynamic-slice_fusion
  352.7 0.1 all-reduce.11.cloned.1.call-update
  352.7 0.0 copy-done.3
  352.8 1.3 dynamic-slice.2
  354.1 0.6 subtract_reduce_fusion
  354.7 29.9 %psum.21 = f32[]{:T(128)} all-reduce(f32[]{:T(128)} %subtract_reduce_fusion), channel_id=1, replica_groups=mesh['grp'=2,'dp_0'=16,'dp_1'=8,'dp_2'=2] {'dp_0'}, use_global_device_ids=true, to_apply=%region_8.9 | all-reduce | flops 1 | bytes 8 | tf_op jit(solution)/shard_map/psum | solution.py:41
  384.6 16.3 %psum.22 = f32[]{:T(128)} all-reduce(f32[]{:T(128)} %psum.21), channel_id=1, replica_groups=mesh['grp'=2,'dp_0'=16,'dp_1'=8,'dp_2'=2] {'dp_1'}, use_global_device_ids=true, to_apply=%region_9.10 | all-reduce | flops 1 | bytes 8 | tf_op jit(solution)/shard_map/psum | solution.py:41
  400.9 3.1 psum.23
  404.6 29.8 %all-reduce.11.cloned.1.call-done = f32[8,3712]{1,0:T(8,128)} async-done(((f32[8,3712]{1,0:T(8,128)}), f32[8,3712]{1,0:T(8,128)}) %all-reduce.11.cloned.1.call-update) | async-done | bytes 118800
  434.4 1.6 fusion.17
  436.0 0.0 copy-done.1
  436.0 0.0 copy-done.2
  436.1 0.6 multiply_add_fusion
  (6 shorter events, 0.1 us)
Async XLA Ops:
  7.2 73.5 %copy-start = (s32[512]{0:T(512)S(1)}, s32[512]{0:T(512)}, u32[]{:S(2)}) copy-start(s32[512]{0:T(512)} %param.10) | copy-start | bytes 6148
  70.3 9.4 %copy-start.4 = (s32[1,256]{1,0:T(1,128)S(1)}, s32[1,256]{1,0:T(1,128)}, u32[]{:S(2)}) copy-start(s32[1,256]{1,0:T(1,128)} %param.11) | copy-start | bytes 3076
  70.3 48.9 %all-to-all-start.1 = ((f32[8,16,3712]{2,1,0:T(8,128)}), f32[8,16,3712]{2,1,0:T(8,128)S(1)}, u32[]{:S(2)}, u32[]{:S(2)}) async-start(f32[8,16,3712]{2,1,0:T(8,128)} %stack.13), calls=%async_computation.1 | async-start | bytes 3801088 | tf_op jit(solution)/shard_map/all_to_all | solution.py:27
  78.2 121.7 %reduce-scatter.2.cloned.1.call-start = ((), (), s32[]{:S(2)}) async-start(), calls=%async_computation.4 | async-start | bytes 5701632 | tf_op jit(solution)/shard_map/reduce_scatter | solution.py:51
  145.4 5.7 %slice-start = ((f32[950272]{0:T(1024)}), f32[10]{0:T(128)S(1)}, s32[]{:S(2)}) async-start(f32[950272]{0:T(1024)} %reshape_reshape.10), calls=%async_computation.7 | async-start | bytes 1024 | tf_op jit(solution)/shard_map/jvp()/slice | solution.py:71
  179.7 173.0 %copy-start.3 = (f32[1,3712]{1,0:T(1,128)S(1)}, f32[1,3712]{1,0:T(1,128)}, u32[]{:S(2)}) copy-start(f32[1,3712]{1,0:T(1,128)} %param.8) | copy-start | bytes 44548
  179.7 256.3 %copy-start.1 = (f32[3712]{0:T(1024)S(1)}, f32[3712]{0:T(1024)}, u32[]{:S(2)}) copy-start(f32[3712]{0:T(1024)} %param.6) | copy-start | bytes 44548
  179.7 256.3 %copy-start.2 = (f32[3712]{0:T(1024)S(1)}, f32[3712]{0:T(1024)}, u32[]{:S(2)}) copy-start(f32[3712]{0:T(1024)} %param.7) | copy-start | bytes 44548
  179.7 171.4 %all-reduce.9.cloned.1.call-start = ((), (), s32[]{:S(2)}) async-start(), calls=%async_computation.5 | async-start | bytes 3801088
  199.9 234.5 %all-reduce.11.cloned.1.call-start = ((), (), s32[]{:S(2)}) async-start(), calls=%async_computation.6 | async-start | bytes 237568
Sparse Core Ops, SparseCore 0:
  179.8 19.9 reduce-scatter.1
  202.3 148.8 all-reduce.8
  353.5 80.9 all-reduce.10
